TPU v7x, 32 devices: a whole 2x2x4 slice. The times are simulated.
32 devices in a mesh: gy: 16 (over z, y, core), gz: 2 (over x).
Axes of the slice: x: 2, y: 2, z: 4, core: 2. Of those that a mesh axis runs over, the one named last changes fastest.
Arguments:
- omega: float32 [3, 256, 128, 128], P(None, 'gy', 'gz'), may hold values from -6 to 6
- velocity: float32 [3, 256, 128, 128], P(None, 'gy', 'gz'), may hold values from -6 to 6
- point_owner: int32 [1152], replicated, may hold values from 0 to 22, as said below
- point_cells: int32 [3, 1152], replicated, may hold values from 1 to 125, as said below
- point_frac: float32 [3, 1152], replicated, may hold values from 0 to 1
- chord: float32 [1152], replicated, may hold values from 0.2 to 1
- twist: float32 [1152], replicated, may hold values from -0.3 to 0.3
- angle_step: int32 [1], replicated, may hold values from 0 to 719
Outputs:
- omega_out: float32 [3, 256, 128, 128], P(None, 'gy', 'gz')
- blade_sources: float32 [3, 1152], replicated
Inputs may be any that keep to these rules, and one draw needn't show every extreme that they name: `point_owner`: turbine t's points lie in spanwise blocks t * 2 to (t + 1) * 2 - 1 and in the 1 vertical blocks from (1) // 2 on; no block holds more than 192 points, and in every turbine one block holds exactly 192. `point_cells`: streamwise cells lie in 1 to 125, spanwise in 1 to 13, vertical in 1 to 61; all points of a turbine share one streamwise cell.
All inputs are finite; a program needn't handle non-finite values.
Results may differ from a plain program's by a relative error of at most 0.0003.
Values sent between devices are 32-bit elements; how exact they have to be, the bound alone decides.
A program may use at most 128 MiB of HBM per device.

v0:
```python
import jax
import jax.numpy as jnp
from jax import lax
from jax.sharding import PartitionSpec as P

TURBINES = 6
BLADES = 3
BP = 64
section_step = 0.4
viscosity = 0.05
tip_speed = 3.0
turn_step = 2.0 * 3.141592653589793 / 720.0


def with_halo(x, sides, width):
    for axis, dim in sides:
        size, length = (lax.axis_size(axis), x.shape[dim])
        up = [(i, (i + 1) % size) for i in range(size - 1)]
        down = [(j, i) for i, j in up]
        last = lax.slice_in_dim(x, length - width, length, axis=dim)
        initial = lax.slice_in_dim(x, 0, width, axis=dim)
        before = lax.ppermute(last, axis, up)
        after = lax.ppermute(initial, axis, down)
        x = jnp.concatenate([before, x, after], axis=dim)
    return x


def remesh_kernel(shift):
    mag = jnp.abs(shift)
    inner = 1.0 - 2.5 * mag * mag + 1.5 * mag * mag * mag
    outer = 0.5 * (2.0 - mag) * (2.0 - mag) * (1.0 - mag)
    return jnp.where(mag < 1.0, inner, jnp.where(mag < 2.0, outer, 0.0))


def shifted(padded, axis, offset):
    index = []
    for dim in range(4):
        if dim == 0:
            index.append(slice(None))
        elif dim == axis:
            index.append(slice(offset, offset + padded.shape[dim] - 4))
        else:
            index.append(slice(2, padded.shape[dim] - 2))
    return padded[tuple(index)]


def centered_first(padded, axis):
    return (
        shifted(padded, axis, 0)
        - 8.0 * shifted(padded, axis, 1)
        + 8.0 * shifted(padded, axis, 3)
        - shifted(padded, axis, 4)
    ) / 12.0


def centered_second(padded, axis):
    return (
        -shifted(padded, axis, 0)
        + 16.0 * shifted(padded, axis, 1)
        - 30.0 * shifted(padded, axis, 2)
        + 16.0 * shifted(padded, axis, 3)
        - shifted(padded, axis, 4)
    ) / 12.0


def remesh_padded(field, displace, axis):
    length = field.shape[axis] - 4
    total = jnp.zeros(field.shape[:axis] + (length,) + field.shape[axis + 1 :], jnp.float32)
    for offset in range(-2, 3):
        start = 2 - offset
        part = lax.slice_in_dim(field, start, start + length, axis=axis)
        moved = lax.slice_in_dim(displace, start, start + length, axis=axis - 1)
        total = total + remesh_kernel(offset - moved)[None] * part
    return total


def blade_forces(point_velocity, chord, twist, angle_step):
    count = point_velocity.shape[1]
    points = jnp.arange(count, dtype=jnp.int32)
    station = points % BP
    blade = points // BP % BLADES
    theta = angle_step[0].astype(
        jnp.float32
    ) * turn_step + 2.0 * 3.141592653589793 / 3.0 * blade.astype(jnp.float32)
    radius = (station.astype(jnp.float32) + 0.5) / BP
    cos_t = jnp.cos(theta)
    sin_t = jnp.sin(theta)
    rel_x = point_velocity[0]
    rel_y = point_velocity[1] + tip_speed * radius * sin_t
    rel_z = point_velocity[2] - tip_speed * radius * cos_t
    rel_t = -sin_t * rel_y + cos_t * rel_z
    speed = jnp.sqrt(rel_x * rel_x + rel_t * rel_t + 1.0)
    gamma = 3.141592653589793 * chord * (rel_x * jnp.cos(twist) + rel_t * jnp.sin(twist))
    blades = gamma.reshape(-1, BP)
    before = jnp.concatenate([jnp.zeros((blades.shape[0], 1), jnp.float32), blades[:, :-1]], axis=1)
    shed = (blades - before).reshape(-1)
    return jnp.stack(
        [
            shed * rel_x / speed,
            gamma * cos_t + shed * rel_y / speed,
            gamma * sin_t + shed * rel_z / speed,
        ]
    )


def point_tables(
    cells,
    fracs,
    owner_span,
    owner_vert,
    span_index,
    vert_index,
    span_cells,
    vert_cells,
    axial_cells,
):
    rows_x = jnp.arange(axial_cells, dtype=jnp.int32)
    rows_y = jnp.arange(span_cells, dtype=jnp.int32)
    rows_z = jnp.arange(vert_cells, dtype=jnp.int32)
    gap_x = rows_x[:, None] - cells[0][None, :]
    gap_y = (
        span_index * span_cells
        + rows_y[:, None]
        - owner_span[None, :] * span_cells
        - cells[1][None, :]
    )
    gap_z = (
        vert_index * vert_cells
        + rows_z[:, None]
        - owner_vert[None, :] * vert_cells
        - cells[2][None, :]
    )
    table_x = remesh_kernel(gap_x.astype(jnp.float32) - fracs[0][None, :])
    table_y = remesh_kernel(gap_y.astype(jnp.float32) - fracs[1][None, :])
    table_z = remesh_kernel(gap_z.astype(jnp.float32) - fracs[2][None, :])
    return (table_x, table_y, table_z)


def on_device(omega, velocity, point_owner, point_cells, point_frac, chord, twist, angle_step):
    span_cells, vert_cells, axial_cells = (omega.shape[1], omega.shape[2], omega.shape[3])
    span_count = lax.axis_size("gy")
    vert_count = lax.axis_size("gz")
    span_index = lax.axis_index("gy")
    vert_index = lax.axis_index("gz")
    owner_span = point_owner // vert_count
    owner_vert = point_owner % vert_count
    highest = lax.Precision.HIGHEST
    busiest = 2 * (BLADES * BP) // (span_count // TURBINES * max(vert_count // 2, 1))
    my_block = span_index * vert_count + vert_index
    points = jnp.arange(point_owner.shape[0], dtype=jnp.int32)
    ranking = jnp.where(point_owner == my_block, points, points + point_owner.shape[0])
    picked = jnp.argsort(ranking, stable=True)[:busiest]
    selector = (picked[:, None] == points[None, :]).astype(jnp.float32)
    table_x, table_y, table_z = point_tables(
        point_cells[:, picked],
        point_frac[:, picked],
        owner_span[picked],
        owner_vert[picked],
        span_index,
        vert_index,
        span_cells,
        vert_cells,
        axial_cells,
    )
    columns = jnp.dot(
        velocity.reshape(-1, axial_cells),
        table_x,
        precision=highest,
        preferred_element_type=jnp.float32,
    )
    columns = columns.reshape(3, span_cells, vert_cells, -1)
    compact = jnp.einsum("cyzq,yq,zq->cq", columns, table_y, table_z, precision=highest)
    partial_velocity = jnp.dot(
        compact, selector, precision=highest, preferred_element_type=jnp.float32
    )
    point_velocity = lax.psum(partial_velocity, ("gy", "gz"))
    sources = blade_forces(point_velocity, chord, twist, angle_step)
    local_sources = sources[:, picked]
    spread = jnp.einsum("cq,yq,zq->cyzq", local_sources, table_y, table_z, precision=highest)
    smear = jnp.dot(
        spread.reshape(-1, spread.shape[3]),
        table_x.T,
        precision=highest,
        preferred_element_type=jnp.float32,
    )
    smear = smear.reshape(3, span_cells, vert_cells, axial_cells)
    omega_rim, velocity_rim = (
        with_halo(omega, (("gy", 1), ("gz", 2)), 2),
        with_halo(velocity, (("gy", 1), ("gz", 2)), 2),
    )
    axial_pads = ((0, 0), (0, 0), (0, 0), (2, 2))
    omega_pad = jnp.pad(omega_rim, axial_pads)
    velocity_pad = jnp.pad(velocity_rim, axial_pads)
    stretch = jnp.zeros_like(omega)
    laplace = jnp.zeros_like(omega)
    for axis in range(3):
        stretch = stretch + omega[2 - axis][None] * centered_first(velocity_pad, 3 - axis)
        laplace = laplace + centered_second(omega_pad, axis + 1)
    section = omega + section_step * (stretch + viscosity * laplace + smear)
    shift_x = jnp.clip(section_step * velocity[0], -1.0, 1.0)
    moved_x = remesh_padded(
        jnp.pad(section, axial_pads), jnp.pad(shift_x, ((0, 0), (0, 0), (2, 2))), 3
    )
    shift_z = jnp.clip(section_step * velocity_rim[2][2 : span_cells + 2, :, :], -1.0, 1.0)
    span_rim = with_halo(moved_x, (("gy", 1),), 2)
    shift_y = jnp.clip(section_step * velocity_rim[1][:, 2 : vert_cells + 2, :], -1.0, 1.0)
    moved_mid = remesh_padded(span_rim, shift_y, 1)
    moved_y = with_halo(moved_mid, (("gz", 2),), 2)
    omega_out = remesh_padded(moved_y, shift_z, 2)
    return (omega_out, sources)


def solution(mesh):
    in_specs = (P(None, "gy", "gz", None), P(None, "gy", "gz", None), P(), P(), P(), P(), P(), P())
    out_specs = (P(None, "gy", "gz", None), P())
    return jax.shard_map(
        on_device, mesh=mesh, in_specs=in_specs, out_specs=out_specs, check_vma=False
    )
```

profile of v0, /device:TPU:10, one launch (start us, length us, event | category | flops | bytes accessed | tf_op | source)
XLA Modules:
  0.0 163.6 jit_solution(6236119518289551892)
XLA Ops:
  0.6 1.8 %fusion.252 = (f32[3,2,64,128]{3,2,1,0:T(8,128)}, f32[3,2,64,128]{3,2,1,0:T(8,128)}) fusion(f32[3,16,64,128]{3,2,1,0:T(8,128)} %param.9), kind=kLoop, calls=%fused_computation.439 | loop fusion | bytes 786432 | tf_op jit(solution)/shard_map/slice | solution.py:21
  2.5 2.0 %collective-permute-start = (f32[3,2,64,128]{3,2,1,0:T(8,128)}, f32[3,2,64,128]{3,2,1,0:T(8,128)}, u32[]{:S(2)}, u32[]{:S(2)}) collective-permute-start(f32[3,2,64,128]{3,2,1,0:T(8,128)} %get-tuple-element.33), channel_id=1, source_target_pairs={{0,2},{2,4},{4,6},{6,8},{8,10},{10,12},{12,14},{14,16},{16,18},{18... | collective-permute-start | bytes 589832 | tf_op jit(solution)/shard_map/ppermute | solution.py:22
  4.5 4.5 %collective-permute-start.1 = (f32[3,2,64,128]{3,2,1,0:T(8,128)}, f32[3,2,64,128]{3,2,1,0:T(8,128)}, u32[]{:S(2)}, u32[]{:S(2)}) collective-permute-start(f32[3,2,64,128]{3,2,1,0:T(8,128)} %get-tuple-element.32), channel_id=1, source_target_pairs={{2,0},{4,2},{6,4},{8,6},{10,8},{12,10},{14,12},{16,14},{18,16},{20... | collective-permute-start | bytes 589832 | tf_op jit(solution)/shard_map/ppermute | solution.py:23
  9.1 1.7 %fusion.253 = (f32[3,2,64,128]{3,2,1,0:T(8,128)S(1)}, f32[3,2,64,128]{3,2,1,0:T(8,128)}) fusion(f32[3,16,64,128]{3,2,1,0:T(8,128)} %param.8), kind=kLoop, calls=%fused_computation.440 | loop fusion | bytes 786432 | tf_op jit(solution)/shard_map/slice | solution.py:21
  10.8 2.0 %collective-permute-start.4 = (f32[3,2,64,128]{3,2,1,0:T(8,128)}, f32[3,2,64,128]{3,2,1,0:T(8,128)}, u32[]{:S(2)}, u32[]{:S(2)}) collective-permute-start(f32[3,2,64,128]{3,2,1,0:T(8,128)} %get-tuple-element.35), channel_id=1, source_target_pairs={{0,2},{2,4},{4,6},{6,8},{8,10},{10,12},{12,14},{14,16},{16,18},{18... | collective-permute-start | bytes 589832 | tf_op jit(solution)/shard_map/ppermute | solution.py:22
  12.8 4.5 %collective-permute-start.5 = (f32[3,2,64,128]{3,2,1,0:T(8,128)S(1)}, f32[3,2,64,128]{3,2,1,0:T(8,128)}, u32[]{:S(2)}, u32[]{:S(2)}) collective-permute-start(f32[3,2,64,128]{3,2,1,0:T(8,128)S(1)} %get-tuple-element.34), channel_id=1, source_target_pairs={{2,0},{4,2},{6,4},{8,6},{10,8},{12,10},{14,12},{16,14},{18,16},{20... | collective-permute-start | bytes 589832 | tf_op jit(solution)/shard_map/ppermute | solution.py:23
  17.4 5.0 %sort.17 = (s32[1152]{0:T(1024)}, s32[1152]{0:T(1024)S(1)}) sort(s32[1152]{0:T(1024)S(1)} %get-tuple-element.63, s32[1152]{0:T(1024)S(1)} %iota.43), dimensions={0}, to_apply=%region_0.1 | sort | flops 12672 | bytes 18432 | tf_op jit(solution)/shard_map/jit(argsort)/sort | solution.py:152
  27.0 3.6 %convolution_bitcast_fusion = f32[3072,192]{0,1:T(8,128)} fusion(f32[3072,128]{1,0:T(8,128)S(1)} %bitcast.49, f32[192]{0:T(256)S(1)} %get-tuple-element.8, s32[192]{0:T(256)S(1)} %get-tuple-element.5), kind=kOutput, calls=%fused_computation.18 | convolution fusion | flops 906461184 | bytes 3933696 | tf_op jit(solution)/shard_map/dot_general | solution.py:165
  30.6 2.2 %copy.29 = f32[3072,192]{1,0:T(8,128)S(1)} copy(f32[3072,192]{0,1:T(8,128)} %convolution_bitcast_fusion) | data formatting | bytes 4718592
  37.2 40.4 %psum.7 = f32[3,1152]{1,0:T(4,128)S(1)} all-reduce(f32[3,1152]{1,0:T(4,128)S(1)} %fusion.77), channel_id=1, replica_groups=mesh['gy'=16,'gz'=2] {'gy','gz'}, use_global_device_ids=true, to_apply=%region_1.2 | all-reduce | flops 3456 | bytes 27648 | tf_op jit(solution)/shard_map/psum | solution.py:176
  83.4 1.7 %gather_fusion.4 = f32[192,3]{1,0:T(8,128)S(1)} fusion(f32[3,1152]{0,1:T(8,128)} %copy.17, s32[1024]{0:T(1024)S(1)} %pad_clamp_fusion), kind=kCustom, calls=%fused_computation.4 | custom fusion | bytes 5376 | tf_op jit(solution)/shard_map/gather | solution.py:178
  85.3 4.3 %fusion.93 = (f32[16,64,128]{2,1,0:T(8,128)}, f32[16,64,128]{2,1,0:T(8,128)}, f32[16,64,128]{2,1,0:T(8,128)}, f32[16,64,128]{2,1,0:T(8,128)}) fusion(f32[16,64,128]{2,1,0:T(8,128)} %get-tuple-element.22), kind=kLoop, calls=%fused_computation.199 | loop fusion | flops 9437184 | bytes 2621440 | tf_op jit(solution)/shard_map/jit(_where)/select_n | solution.py:32
  94.4 4.7 %collective-permute-start.3 = (f32[3,20,2,128]{3,2,1,0:T(2,128)S(1)}, f32[3,20,2,128]{3,2,1,0:T(2,128)S(1)}, u32[]{:S(2)}, u32[]{:S(2)}) collective-permute-start(f32[3,20,2,128]{3,2,1,0:T(2,128)S(1)} %get-tuple-element.14), channel_id=1, source_target_pairs={{1,0},{3,2},{5,4},{7,6},{9,8},{11,10},{13,12},{15,14},{17,16},{19,... | collective-permute-start | bytes 184328 | tf_op jit(solution)/shard_map/ppermute | solution.py:23
  103.3 4.5 %collective-permute-start.7 = (f32[3,20,2,128]{3,2,1,0:T(2,128)S(1)}, f32[3,20,2,128]{3,2,1,0:T(2,128)S(1)}, u32[]{:S(2)}, u32[]{:S(2)}) collective-permute-start(f32[3,20,2,128]{3,2,1,0:T(2,128)S(1)} %get-tuple-element.16), channel_id=1, source_target_pairs={{1,0},{3,2},{5,4},{7,6},{9,8},{11,10},{13,12},{15,14},{17,16},{19,... | collective-permute-start | bytes 184328 | tf_op jit(solution)/shard_map/ppermute | solution.py:23
  107.9 1.7 %pad_maximum_fusion = f32[3,20,68,128]{3,2,1,0:T(8,128)} fusion(f32[3,20,2,128]{3,2,1,0:T(2,128)S(1)} %collective-permute-done.3, f32[3,20,64,128]{3,2,1,0:T(8,128)S(1)} %get-tuple-element.53, f32[3,20,2,128]{3,2,1,0:T(2,128)S(1)} %collective-permute-done.2), kind=kLoop, calls=%fused_computation.23 | loop fusion | flops 1044480 | bytes 4177920 | tf_op jit(solution)/shard_map/concatenate | solution.py:24
  110.8 3.5 %select_maximum_fusion = f32[3,20,68,132]{3,2,1,0:T(8,128)} fusion(f32[3,20,2,128]{3,2,1,0:T(2,128)S(1)} %collective-permute-done.7, f32[3,20,64,128]{3,2,1,0:T(8,128)S(1)} %get-tuple-element.57, f32[3,20,2,128]{3,2,1,0:T(2,128)S(1)} %collective-permute-done.6), kind=kLoop, calls=%fused_computation.15 | loop fusion | flops 4308480 | bytes 4243200 | tf_op jit(solution)/shard_map/concatenate | solution.py:24
  114.4 20.4 %fusion.30 = f32[3,16,64,128]{3,2,1,0:T(8,128)} fusion(f32[3,16,64,128]{3,2,1,0:T(8,128)S(1)} %copy-done.2, f32[3,20,64,128]{3,2,1,0:T(8,128)} %copy-done.4, f32[3,20,2,128]{3,2,1,0:T(2,128)S(1)} %collective-permute-done.7, f32[3,20,2,128]{3,2,1,0:T(2,128)S(1)} %collective-permute-done.6, f32[3,20,64,128]{3,2,1,0:T(8,128)} %copy-done.3, ...), kind=kOutput, calls=%fused_computation.70 | convolution fusion | flops 929464320 | bytes 29947392 | tf_op jit(solution)/shard_map/dot_general | solution.py:180
  134.7 6.4 %fusion.48 = f32[3,16,64,128]{3,2,1,0:T(8,128)S(1)} fusion(f32[3,16,64,128]{3,2,1,0:T(8,128)} %fusion.30, f32[16,64,128]{2,1,0:T(8,128)} %get-tuple-element.49, f32[16,64,128]{2,1,0:T(8,128)} %get-tuple-element.48, f32[16,64,128]{2,1,0:T(8,128)S(1)} %copy-done.5, f32[16,64,128]{2,1,0:T(8,128)} %get-tuple-element.47, f32[16,64,128]{2,1,0:T(8,128)} %get-tuple-element.46), kind=kLoop, calls=%fused_computation.88 | loop fusion | flops 3538944 | bytes 5767168 | tf_op jit(solution)/shard_map/add | solution.py:73
  141.2 1.9 %collective-permute-start.8 = (f32[3,2,64,128]{3,2,1,0:T(8,128)S(1)}, f32[3,2,64,128]{3,2,1,0:T(8,128)S(1)}, u32[]{:S(2)}, u32[]{:S(2)}) collective-permute-start(f32[3,2,64,128]{3,2,1,0:T(8,128)S(1)} %get-tuple-element.19), channel_id=1, source_target_pairs={{2,0},{4,2},{6,4},{8,6},{10,8},{12,10},{14,12},{16,14},{18,16},{20... | collective-permute-start | bytes 589832 | tf_op jit(solution)/shard_map/ppermute | solution.py:23
  143.1 2.4 %collective-permute-start.9 = (f32[3,2,64,128]{3,2,1,0:T(8,128)S(1)}, f32[3,2,64,128]{3,2,1,0:T(8,128)S(1)}, u32[]{:S(2)}, u32[]{:S(2)}) collective-permute-start(f32[3,2,64,128]{3,2,1,0:T(8,128)S(1)} %get-tuple-element.20), channel_id=1, source_target_pairs={{0,2},{2,4},{4,6},{6,8},{8,10},{10,12},{12,14},{14,16},{16,18},{18... | collective-permute-start | bytes 589832 | tf_op jit(solution)/shard_map/ppermute | solution.py:22
  148.3 2.7 %collective-permute-done.9 = f32[3,2,64,128]{3,2,1,0:T(8,128)S(1)} collective-permute-done((f32[3,2,64,128]{3,2,1,0:T(8,128)S(1)}, f32[3,2,64,128]{3,2,1,0:T(8,128)S(1)}, u32[]{:S(2)}, u32[]{:S(2)}) %collective-permute-start.9) | collective-permute-done | bytes 196640 | tf_op jit(solution)/shard_map/ppermute | solution.py:22
  152.4 3.1 %collective-permute-start.10 = (f32[3,16,2,128]{3,2,1,0:T(2,128)S(1)}, f32[3,16,2,128]{3,2,1,0:T(2,128)S(1)}, u32[]{:S(2)}, u32[]{:S(2)}) collective-permute-start(f32[3,16,2,128]{3,2,1,0:T(2,128)S(1)} %get-tuple-element.17), channel_id=1, source_target_pairs={{1,0},{3,2},{5,4},{7,6},{9,8},{11,10},{13,12},{15,14},{17,16},{19,... | collective-permute-start | bytes 147464 | tf_op jit(solution)/shard_map/ppermute | solution.py:23
  158.5 3.0 %collective-permute-done.11 = f32[3,16,2,128]{3,2,1,0:T(2,128)S(1)} collective-permute-done((f32[3,16,2,128]{3,2,1,0:T(2,128)S(1)}, f32[3,16,2,128]{3,2,1,0:T(2,128)S(1)}, u32[]{:S(2)}, u32[]{:S(2)}) %collective-permute-start.11) | collective-permute-done | bytes 49184 | tf_op jit(solution)/shard_map/ppermute | solution.py:22
  161.5 2.1 %fusion.7 = f32[3,16,64,128]{3,2,1,0:T(8,128)} fusion(f32[3,16,2,128]{3,2,1,0:T(2,128)S(1)} %collective-permute-done.11, f32[3,16,64,128]{3,2,1,0:T(8,128)S(1)} %fusion.15, f32[3,16,2,128]{3,2,1,0:T(2,128)S(1)} %collective-permute-done.10, f32[16,64,128]{2,1,0:T(8,128)S(1)} %get-tuple-element.42, f32[16,64,128]{2,1,0:T(8,128)S(1)} %get-tuple-element.43, ...), kind=kLoop, calls=%fused_computation.47 | loop fusion | flops 5111808 | bytes 5865472 | tf_op jit(solution)/shard_map/add | solution.py:73
  (110 shorter events, 31.0 us)
Async XLA Ops:
  0.6 16.8 %copy-start.16 = (s32[1152]{0:T(1024)S(1)}, s32[1152]{0:T(1024)}, u32[]{:S(2)}) copy-start(s32[1152]{0:T(1024)} %param.10) | copy-start | bytes 13828
  0.6 23.3 %copy-start.12 = (s32[3,1152]{1,0:T(4,128)S(1)}, s32[3,1152]{1,0:T(4,128)}, u32[]{:S(2)}) copy-start(s32[3,1152]{1,0:T(4,128)} %param.11) | copy-start | bytes 41476
  2.5 22.8 %copy-start.13 = (f32[3,1152]{1,0:T(4,128)S(1)}, f32[3,1152]{1,0:T(4,128)}, u32[]{:S(2)}) copy-start(f32[3,1152]{1,0:T(4,128)} %param.12) | copy-start | bytes 41476
  2.5 87.8 %collective-permute-start = (f32[3,2,64,128]{3,2,1,0:T(8,128)}, f32[3,2,64,128]{3,2,1,0:T(8,128)}, u32[]{:S(2)}, u32[]{:S(2)}) collective-permute-start(f32[3,2,64,128]{3,2,1,0:T(8,128)} %get-tuple-element.33), channel_id=1, source_target_pairs={{0,2},{2,4},{4,6},{6,8},{8,10},{10,12},{12,14},{14,16},{16,18},{18... | collective-permute-start | bytes 589832 | tf_op jit(solution)/shard_map/ppermute | solution.py:22
  4.5 87.3 %collective-permute-start.1 = (f32[3,2,64,128]{3,2,1,0:T(8,128)}, f32[3,2,64,128]{3,2,1,0:T(8,128)}, u32[]{:S(2)}, u32[]{:S(2)}) collective-permute-start(f32[3,2,64,128]{3,2,1,0:T(8,128)} %get-tuple-element.32), channel_id=1, source_target_pairs={{2,0},{4,2},{6,4},{8,6},{10,8},{12,10},{14,12},{16,14},{18,16},{20... | collective-permute-start | bytes 589832 | tf_op jit(solution)/shard_map/ppermute | solution.py:23
  10.8 16.2 %copy-start = (f32[3,16,64,128]{3,2,1,0:T(8,128)S(1)}, f32[3,16,64,128]{3,2,1,0:T(8,128)}, u32[]{:S(2)}) copy-start(f32[3,16,64,128]{3,2,1,0:T(8,128)} %param.9) | copy-start | bytes 4718596
  10.8 88.3 %collective-permute-start.4 = (f32[3,2,64,128]{3,2,1,0:T(8,128)}, f32[3,2,64,128]{3,2,1,0:T(8,128)}, u32[]{:S(2)}, u32[]{:S(2)}) collective-permute-start(f32[3,2,64,128]{3,2,1,0:T(8,128)} %get-tuple-element.35), channel_id=1, source_target_pairs={{0,2},{2,4},{4,6},{6,8},{8,10},{10,12},{12,14},{14,16},{16,18},{18... | collective-permute-start | bytes 589832 | tf_op jit(solution)/shard_map/ppermute | solution.py:22
  12.8 87.8 %collective-permute-start.5 = (f32[3,2,64,128]{3,2,1,0:T(8,128)S(1)}, f32[3,2,64,128]{3,2,1,0:T(8,128)}, u32[]{:S(2)}, u32[]{:S(2)}) collective-permute-start(f32[3,2,64,128]{3,2,1,0:T(8,128)S(1)} %get-tuple-element.34), channel_id=1, source_target_pairs={{2,0},{4,2},{6,4},{8,6},{10,8},{12,10},{14,12},{16,14},{18,16},{20... | collective-permute-start | bytes 589832 | tf_op jit(solution)/shard_map/ppermute | solution.py:23
  33.4 44.9 %copy-start.14 = (f32[1152]{0:T(1024)S(1)}, f32[1152]{0:T(1024)}, u32[]{:S(2)}) copy-start(f32[1152]{0:T(1024)} %param.14) | copy-start | bytes 13828
  33.4 44.9 %copy-start.15 = (f32[1152]{0:T(1024)S(1)}, f32[1152]{0:T(1024)}, u32[]{:S(2)}) copy-start(f32[1152]{0:T(1024)} %param.13) | copy-start | bytes 13828
  33.4 45.3 %copy-start.2 = (f32[3,16,64,128]{3,2,1,0:T(8,128)S(1)}, f32[3,16,64,128]{3,2,1,0:T(8,128)}, u32[]{:S(2)}) copy-start(f32[3,16,64,128]{3,2,1,0:T(8,128)} %param.8) | copy-start | bytes 4718596
  93.0 16.6 %copy-start.3 = (f32[3,20,64,128]{3,2,1,0:T(8,128)}, f32[3,20,64,128]{3,2,1,0:T(8,128)S(1)}, u32[]{:S(2)}) copy-start(f32[3,20,64,128]{3,2,1,0:T(8,128)S(1)} %get-tuple-element.53) | copy-start | bytes 5898244
  93.1 14.8 %collective-permute-start.2 = (f32[3,20,2,128]{3,2,1,0:T(2,128)S(1)}, f32[3,20,2,128]{3,2,1,0:T(2,128)S(1)}, u32[]{:S(2)}, u32[]{:S(2)}) collective-permute-start(f32[3,20,2,128]{3,2,1,0:T(2,128)S(1)} %get-tuple-element.13), channel_id=1, source_target_pairs={{0,1},{2,3},{4,5},{6,7},{8,9},{10,11},{12,13},{14,15},{16,17},{18,... | collective-permute-start | bytes 184328 | tf_op jit(solution)/shard_map/ppermute | solution.py:22
  94.4 13.5 %collective-permute-start.3 = (f32[3,20,2,128]{3,2,1,0:T(2,128)S(1)}, f32[3,20,2,128]{3,2,1,0:T(2,128)S(1)}, u32[]{:S(2)}, u32[]{:S(2)}) collective-permute-start(f32[3,20,2,128]{3,2,1,0:T(2,128)S(1)} %get-tuple-element.14), channel_id=1, source_target_pairs={{1,0},{3,2},{5,4},{7,6},{9,8},{11,10},{13,12},{15,14},{17,16},{19,... | collective-permute-start | bytes 184328 | tf_op jit(solution)/shard_map/ppermute | solution.py:23
  100.7 13.7 %copy-start.11 = (f32[3,18,64,128]{3,2,1,0:T(8,128)}, f32[3,18,64,128]{3,2,1,0:T(8,128)S(1)}, u32[]{:S(2)}) copy-start(f32[3,18,64,128]{3,2,1,0:T(8,128)S(1)} %get-tuple-element.29) | copy-start | bytes 5308420
  101.9 7.7 %copy-start.7 = (f32[3,18,64,128]{3,2,1,0:T(8,128)}, f32[3,18,64,128]{3,2,1,0:T(8,128)S(1)}, u32[]{:S(2)}) copy-start(f32[3,18,64,128]{3,2,1,0:T(8,128)S(1)} %get-tuple-element.56) | copy-start | bytes 5308420
  101.9 8.9 %copy-start.4 = (f32[3,20,64,128]{3,2,1,0:T(8,128)}, f32[3,20,64,128]{3,2,1,0:T(8,128)S(1)}, u32[]{:S(2)}) copy-start(f32[3,20,64,128]{3,2,1,0:T(8,128)S(1)} %get-tuple-element.57) | copy-start | bytes 5898244
  102.0 8.8 %collective-permute-start.6 = (f32[3,20,2,128]{3,2,1,0:T(2,128)S(1)}, f32[3,20,2,128]{3,2,1,0:T(2,128)S(1)}, u32[]{:S(2)}, u32[]{:S(2)}) collective-permute-start(f32[3,20,2,128]{3,2,1,0:T(2,128)S(1)} %get-tuple-element.15), channel_id=1, source_target_pairs={{0,1},{2,3},{4,5},{6,7},{8,9},{10,11},{12,13},{14,15},{16,17},{18,... | collective-permute-start | bytes 184328 | tf_op jit(solution)/shard_map/ppermute | solution.py:22
  103.3 7.5 %collective-permute-start.7 = (f32[3,20,2,128]{3,2,1,0:T(2,128)S(1)}, f32[3,20,2,128]{3,2,1,0:T(2,128)S(1)}, u32[]{:S(2)}, u32[]{:S(2)}) collective-permute-start(f32[3,20,2,128]{3,2,1,0:T(2,128)S(1)} %get-tuple-element.16), channel_id=1, source_target_pairs={{1,0},{3,2},{5,4},{7,6},{9,8},{11,10},{13,12},{15,14},{17,16},{19,... | collective-permute-start | bytes 184328 | tf_op jit(solution)/shard_map/ppermute | solution.py:23
  114.4 20.4 %copy-start.5 = (f32[16,64,128]{2,1,0:T(8,128)S(1)}, f32[16,64,128]{2,1,0:T(8,128)}, u32[]{:S(2)}) copy-start(f32[16,64,128]{2,1,0:T(8,128)} %get-tuple-element.21) | copy-start | bytes 1572868
  141.2 7.1 %collective-permute-start.8 = (f32[3,2,64,128]{3,2,1,0:T(8,128)S(1)}, f32[3,2,64,128]{3,2,1,0:T(8,128)S(1)}, u32[]{:S(2)}, u32[]{:S(2)}) collective-permute-start(f32[3,2,64,128]{3,2,1,0:T(8,128)S(1)} %get-tuple-element.19), channel_id=1, source_target_pairs={{2,0},{4,2},{6,4},{8,6},{10,8},{12,10},{14,12},{16,14},{18,16},{20... | collective-permute-start | bytes 589832 | tf_op jit(solution)/shard_map/ppermute | solution.py:23
  143.1 7.9 %collective-permute-start.9 = (f32[3,2,64,128]{3,2,1,0:T(8,128)S(1)}, f32[3,2,64,128]{3,2,1,0:T(8,128)S(1)}, u32[]{:S(2)}, u32[]{:S(2)}) collective-permute-start(f32[3,2,64,128]{3,2,1,0:T(8,128)S(1)} %get-tuple-element.20), channel_id=1, source_target_pairs={{0,2},{2,4},{4,6},{6,8},{8,10},{10,12},{12,14},{14,16},{16,18},{18... | collective-permute-start | bytes 589832 | tf_op jit(solution)/shard_map/ppermute | solution.py:22
  152.4 6.1 %collective-permute-start.10 = (f32[3,16,2,128]{3,2,1,0:T(2,128)S(1)}, f32[3,16,2,128]{3,2,1,0:T(2,128)S(1)}, u32[]{:S(2)}, u32[]{:S(2)}) collective-permute-start(f32[3,16,2,128]{3,2,1,0:T(2,128)S(1)} %get-tuple-element.17), channel_id=1, source_target_pairs={{1,0},{3,2},{5,4},{7,6},{9,8},{11,10},{13,12},{15,14},{17,16},{19,... | collective-permute-start | bytes 147464 | tf_op jit(solution)/shard_map/ppermute | solution.py:23
  155.5 6.0 %collective-permute-start.11 = (f32[3,16,2,128]{3,2,1,0:T(2,128)S(1)}, f32[3,16,2,128]{3,2,1,0:T(2,128)S(1)}, u32[]{:S(2)}, u32[]{:S(2)}) collective-permute-start(f32[3,16,2,128]{3,2,1,0:T(2,128)S(1)} %get-tuple-element.18), channel_id=1, source_target_pairs={{0,1},{2,3},{4,5},{6,7},{8,9},{10,11},{12,13},{14,15},{16,17},{18,... | collective-permute-start | bytes 147464 | tf_op jit(solution)/shard_map/ppermute | solution.py:22
  (9 other events, 35.2 us)
where the time goes:
time: 164 us
  blocking collectives  40.4 us (25%)
  starting transfers between devices  33.8 us (21%)
  other arithmetic  33.1 us (20%)
  matrix products  25.8 us (16%)
  local copies, waits for them, and re-layouts  22.7 us (14%)
  waiting for transfers between devices  5.74 us (4%)
  between operations  1.99 us (1%)
    psum x1, blocking collectives, on_device(): point_velocity = lax.psum(partial_velocity, ('gy', 'gz'))  40.4 us
    ppermute x6, starting transfers between devices, with_halo(): after = lax.ppermute(initial, axis, down)  23.4 us
    dot_general x1, matrix products, on_device(): jnp.dot(spread.reshape(-1, spread.shape[3]), table_x.T, precision=highest...  20.4 us
    ppermute x6, starting transfers between devices, with_halo(): before = lax.ppermute(last, axis, up)  10.4 us
    add x3, other arithmetic, remesh_padded(): total = total + remesh_kernel(offset - moved)[None] * part  9.8 us
    select_n x4, other arithmetic, remesh_kernel(): return jnp.where(mag < 1.0, inner, jnp.where(mag < 2.0, outer, 0.0))  7.58 us
    unnamed x47, local copies, waits for them, and re-layouts  6.02 us
    ppermute x6, waiting for transfers between devices, with_halo(): before = lax.ppermute(last, axis, up)  5.72 us
  transfers between devices with their start and end apart: 12, of which 2 were waited for; matrix products, arithmetic and copies ran while one was open for 27% of the time, Pallas kernels for 0%

commit v1 on v0

--- a/solution.py
+++ b/solution.py
@@ -173,7 +173,7 @@
     partial_velocity = jnp.dot(
         compact, selector, precision=highest, preferred_element_type=jnp.float32
     )
-    point_velocity = lax.psum(partial_velocity, ("gy", "gz"))
+    point_velocity = lax.psum(lax.psum(partial_velocity, "gz"), "gy")
     sources = blade_forces(point_velocity, chord, twist, angle_step)
     local_sources = sources[:, picked]
     spread = jnp.einsum("cq,yq,zq->cyzq", local_sources, table_y, table_z, precision=highest)

time: 164 us -> 187 us (1.14)
  the two profiles are of different devices: /device:TPU:10 before, /device:TPU:6 now
where the time goes in v1:
time: 187 us; the launch traced here: 186 us
  blocking collectives  61.9 us (33%)
  other arithmetic  33.2 us (18%)
  starting transfers between devices  32 us (17%)
  matrix products  26 us (14%)
  local copies, waits for them, and re-layouts  22.8 us (12%)
  waiting for transfers between devices  8.16 us (4%)
  between operations  1.99 us (1%)
    psum x2, blocking collectives, on_device(): point_velocity = lax.psum(lax.psum(partial_velocity, 'gz'), 'gy')  61.9 us
    ppermute x6, starting transfers between devices, with_halo(): after = lax.ppermute(initial, axis, down)  21.6 us
    dot_general x1, matrix products, on_device(): jnp.dot(spread.reshape(-1, spread.shape[3]), table_x.T, precision=highest...  20.6 us
    ppermute x6, starting transfers between devices, with_halo(): before = lax.ppermute(last, axis, up)  10.4 us
    add x3, other arithmetic, remesh_padded(): total = total + remesh_kernel(offset - moved)[None] * part  9.82 us
    ppermute x6, waiting for transfers between devices, with_halo(): before = lax.ppermute(last, axis, up)  8.15 us
    select_n x4, other arithmetic, remesh_kernel(): return jnp.where(mag < 1.0, inner, jnp.where(mag < 2.0, outer, 0.0))  7.59 us
    unnamed x47, local copies, waits for them, and re-layouts  6.05 us
  transfers between devices with their start and end apart: 12, of which 2 were waited for; matrix products, arithmetic and copies ran while one was open for 24% of the time, Pallas kernels for 0%

profile of v1, /device:TPU:6, one launch (start us, length us, event | category | flops | bytes accessed | tf_op | source)
XLA Modules:
  0.0 185.9 jit_solution(11465948127642026870)
XLA Ops:
  0.6 1.8 fusion.252
  2.5 2.0 %collective-permute-start = (f32[3,2,64,128]{3,2,1,0:T(8,128)}, f32[3,2,64,128]{3,2,1,0:T(8,128)}, u32[]{:S(2)}, u32[]{:S(2)}) collective-permute-start(f32[3,2,64,128]{3,2,1,0:T(8,128)} %get-tuple-element.33), channel_id=1, source_target_pairs={{0,2},{2,4},{4,6},{6,8},{8,10},{10,12},{12,14},{14,16},{16,18},{18... | collective-permute-start | bytes 589832 | tf_op jit(solution)/shard_map/ppermute | solution.py:22
  4.5 3.6 %collective-permute-start.1 = (f32[3,2,64,128]{3,2,1,0:T(8,128)}, f32[3,2,64,128]{3,2,1,0:T(8,128)}, u32[]{:S(2)}, u32[]{:S(2)}) collective-permute-start(f32[3,2,64,128]{3,2,1,0:T(8,128)} %get-tuple-element.32), channel_id=1, source_target_pairs={{2,0},{4,2},{6,4},{8,6},{10,8},{12,10},{14,12},{16,14},{18,16},{20... | collective-permute-start | bytes 589832 | tf_op jit(solution)/shard_map/ppermute | solution.py:23
  9.9 2.0 %collective-permute-start.4 = (f32[3,2,64,128]{3,2,1,0:T(8,128)}, f32[3,2,64,128]{3,2,1,0:T(8,128)}, u32[]{:S(2)}, u32[]{:S(2)}) collective-permute-start(f32[3,2,64,128]{3,2,1,0:T(8,128)} %get-tuple-element.35), channel_id=1, source_target_pairs={{0,2},{2,4},{4,6},{6,8},{8,10},{10,12},{12,14},{14,16},{16,18},{18... | collective-permute-start | bytes 589832 | tf_op jit(solution)/shard_map/ppermute | solution.py:22
  11.9 3.6 %collective-permute-start.5 = (f32[3,2,64,128]{3,2,1,0:T(8,128)S(1)}, f32[3,2,64,128]{3,2,1,0:T(8,128)}, u32[]{:S(2)}, u32[]{:S(2)}) collective-permute-start(f32[3,2,64,128]{3,2,1,0:T(8,128)S(1)} %get-tuple-element.34), channel_id=1, source_target_pairs={{2,0},{4,2},{6,4},{8,6},{10,8},{12,10},{14,12},{16,14},{18,16},{20... | collective-permute-start | bytes 589832 | tf_op jit(solution)/shard_map/ppermute | solution.py:23
  15.7 5.0 %sort.17 = (s32[1152]{0:T(1024)}, s32[1152]{0:T(1024)S(1)}) sort(s32[1152]{0:T(1024)S(1)} %get-tuple-element.63, s32[1152]{0:T(1024)S(1)} %iota.43), dimensions={0}, to_apply=%region_0.1 | sort | flops 12672 | bytes 18432 | tf_op jit(solution)/shard_map/jit(argsort)/sort | solution.py:152
  25.3 3.5 %convolution_bitcast_fusion = f32[3072,192]{0,1:T(8,128)} fusion(f32[3072,128]{1,0:T(8,128)S(1)} %bitcast.49, f32[192]{0:T(256)S(1)} %get-tuple-element.8, s32[192]{0:T(256)S(1)} %get-tuple-element.5), kind=kOutput, calls=%fused_computation.18 | convolution fusion | flops 906461184 | bytes 3933696 | tf_op jit(solution)/shard_map/dot_general | solution.py:165
  28.8 2.2 %copy.29 = f32[3072,192]{1,0:T(8,128)S(1)} copy(f32[3072,192]{0,1:T(8,128)} %convolution_bitcast_fusion) | data formatting | bytes 4718592
  35.4 7.3 %psum.14 = f32[3,1152]{1,0:T(4,128)S(1)} all-reduce(f32[3,1152]{1,0:T(4,128)S(1)} %fusion.77), channel_id=1, replica_groups=mesh['gy'=16,'gz'=2] {'gz'}, use_global_device_ids=true, to_apply=%region_1.2 | all-reduce | flops 3456 | bytes 27648 | tf_op jit(solution)/shard_map/psum | solution.py:176
  42.7 54.6 %psum.15 = f32[3,1152]{1,0:T(4,128)S(1)} all-reduce(f32[3,1152]{1,0:T(4,128)S(1)} %psum.14), channel_id=1, replica_groups=mesh['gy'=16,'gz'=2] {'gy'}, use_global_device_ids=true, to_apply=%region_2.3 | all-reduce | flops 3456 | bytes 27648 | tf_op jit(solution)/shard_map/psum | solution.py:176
  103.2 1.7 gather_fusion.4
  105.0 4.3 %fusion.93 = (f32[16,64,128]{2,1,0:T(8,128)}, f32[16,64,128]{2,1,0:T(8,128)}, f32[16,64,128]{2,1,0:T(8,128)}, f32[16,64,128]{2,1,0:T(8,128)}) fusion(f32[16,64,128]{2,1,0:T(8,128)} %get-tuple-element.22), kind=kLoop, calls=%fused_computation.199 | loop fusion | flops 9437184 | bytes 2621440 | tf_op jit(solution)/shard_map/jit(_where)/select_n | solution.py:32
  114.1 4.7 %collective-permute-start.3 = (f32[3,20,2,128]{3,2,1,0:T(2,128)S(1)}, f32[3,20,2,128]{3,2,1,0:T(2,128)S(1)}, u32[]{:S(2)}, u32[]{:S(2)}) collective-permute-start(f32[3,20,2,128]{3,2,1,0:T(2,128)S(1)} %get-tuple-element.14), channel_id=1, source_target_pairs={{1,0},{3,2},{5,4},{7,6},{9,8},{11,10},{13,12},{15,14},{17,16},{19,... | collective-permute-start | bytes 184328 | tf_op jit(solution)/shard_map/ppermute | solution.py:23
  123.0 4.5 %collective-permute-start.7 = (f32[3,20,2,128]{3,2,1,0:T(2,128)S(1)}, f32[3,20,2,128]{3,2,1,0:T(2,128)S(1)}, u32[]{:S(2)}, u32[]{:S(2)}) collective-permute-start(f32[3,20,2,128]{3,2,1,0:T(2,128)S(1)} %get-tuple-element.16), channel_id=1, source_target_pairs={{1,0},{3,2},{5,4},{7,6},{9,8},{11,10},{13,12},{15,14},{17,16},{19,... | collective-permute-start | bytes 184328 | tf_op jit(solution)/shard_map/ppermute | solution.py:23
  127.6 1.7 pad_maximum_fusion
  130.6 3.5 %select_maximum_fusion = f32[3,20,68,132]{3,2,1,0:T(8,128)} fusion(f32[3,20,2,128]{3,2,1,0:T(2,128)S(1)} %collective-permute-done.7, f32[3,20,64,128]{3,2,1,0:T(8,128)S(1)} %get-tuple-element.57, f32[3,20,2,128]{3,2,1,0:T(2,128)S(1)} %collective-permute-done.6), kind=kLoop, calls=%fused_computation.15 | loop fusion | flops 4308480 | bytes 4243200 | tf_op jit(solution)/shard_map/concatenate | solution.py:24
  134.1 20.6 %fusion.30 = f32[3,16,64,128]{3,2,1,0:T(8,128)} fusion(f32[3,16,64,128]{3,2,1,0:T(8,128)S(1)} %copy-done.2, f32[3,20,64,128]{3,2,1,0:T(8,128)} %copy-done.4, f32[3,20,2,128]{3,2,1,0:T(2,128)S(1)} %collective-permute-done.7, f32[3,20,2,128]{3,2,1,0:T(2,128)S(1)} %collective-permute-done.6, f32[3,20,64,128]{3,2,1,0:T(8,128)} %copy-done.3, ...), kind=kOutput, calls=%fused_computation.70 | convolution fusion | flops 929464320 | bytes 29947392 | tf_op jit(solution)/shard_map/dot_general | solution.py:180
  154.7 6.4 %fusion.48 = f32[3,16,64,128]{3,2,1,0:T(8,128)S(1)} fusion(f32[3,16,64,128]{3,2,1,0:T(8,128)} %fusion.30, f32[16,64,128]{2,1,0:T(8,128)} %get-tuple-element.49, f32[16,64,128]{2,1,0:T(8,128)} %get-tuple-element.48, f32[16,64,128]{2,1,0:T(8,128)S(1)} %copy-done.5, f32[16,64,128]{2,1,0:T(8,128)} %get-tuple-element.47, f32[16,64,128]{2,1,0:T(8,128)} %get-tuple-element.46), kind=kLoop, calls=%fused_computation.88 | loop fusion | flops 3538944 | bytes 5767168 | tf_op jit(solution)/shard_map/add | solution.py:73
  161.1 1.9 %collective-permute-start.8 = (f32[3,2,64,128]{3,2,1,0:T(8,128)S(1)}, f32[3,2,64,128]{3,2,1,0:T(8,128)S(1)}, u32[]{:S(2)}, u32[]{:S(2)}) collective-permute-start(f32[3,2,64,128]{3,2,1,0:T(8,128)S(1)} %get-tuple-element.19), channel_id=1, source_target_pairs={{2,0},{4,2},{6,4},{8,6},{10,8},{12,10},{14,12},{16,14},{18,16},{20... | collective-permute-start | bytes 589832 | tf_op jit(solution)/shard_map/ppermute | solution.py:23
  163.1 2.4 %collective-permute-start.9 = (f32[3,2,64,128]{3,2,1,0:T(8,128)S(1)}, f32[3,2,64,128]{3,2,1,0:T(8,128)S(1)}, u32[]{:S(2)}, u32[]{:S(2)}) collective-permute-start(f32[3,2,64,128]{3,2,1,0:T(8,128)S(1)} %get-tuple-element.20), channel_id=1, source_target_pairs={{0,2},{2,4},{4,6},{6,8},{8,10},{10,12},{12,14},{14,16},{16,18},{18... | collective-permute-start | bytes 589832 | tf_op jit(solution)/shard_map/ppermute | solution.py:22
  168.3 5.1 %collective-permute-done.9 = f32[3,2,64,128]{3,2,1,0:T(8,128)S(1)} collective-permute-done((f32[3,2,64,128]{3,2,1,0:T(8,128)S(1)}, f32[3,2,64,128]{3,2,1,0:T(8,128)S(1)}, u32[]{:S(2)}, u32[]{:S(2)}) %collective-permute-start.9) | collective-permute-done | bytes 196640 | tf_op jit(solution)/shard_map/ppermute | solution.py:22
  174.8 3.1 %collective-permute-start.10 = (f32[3,16,2,128]{3,2,1,0:T(2,128)S(1)}, f32[3,16,2,128]{3,2,1,0:T(2,128)S(1)}, u32[]{:S(2)}, u32[]{:S(2)}) collective-permute-start(f32[3,16,2,128]{3,2,1,0:T(2,128)S(1)} %get-tuple-element.17), channel_id=1, source_target_pairs={{1,0},{3,2},{5,4},{7,6},{9,8},{11,10},{13,12},{15,14},{17,16},{19,... | collective-permute-start | bytes 147464 | tf_op jit(solution)/shard_map/ppermute | solution.py:23
  180.8 3.0 %collective-permute-done.11 = f32[3,16,2,128]{3,2,1,0:T(2,128)S(1)} collective-permute-done((f32[3,16,2,128]{3,2,1,0:T(2,128)S(1)}, f32[3,16,2,128]{3,2,1,0:T(2,128)S(1)}, u32[]{:S(2)}, u32[]{:S(2)}) %collective-permute-start.11) | collective-permute-done | bytes 49184 | tf_op jit(solution)/shard_map/ppermute | solution.py:22
  183.9 2.1 %fusion.7 = f32[3,16,64,128]{3,2,1,0:T(8,128)} fusion(f32[3,16,2,128]{3,2,1,0:T(2,128)S(1)} %collective-permute-done.11, f32[3,16,64,128]{3,2,1,0:T(8,128)S(1)} %fusion.15, f32[3,16,2,128]{3,2,1,0:T(2,128)S(1)} %collective-permute-done.10, f32[16,64,128]{2,1,0:T(8,128)S(1)} %get-tuple-element.42, f32[16,64,128]{2,1,0:T(8,128)S(1)} %get-tuple-element.43, ...), kind=kLoop, calls=%fused_computation.47 | loop fusion | flops 5111808 | bytes 5865472 | tf_op jit(solution)/shard_map/add | solution.py:73
  (111 shorter events, 32.8 us)
Async XLA Ops:
  0.6 15.0 %copy-start.16 = (s32[1152]{0:T(1024)S(1)}, s32[1152]{0:T(1024)}, u32[]{:S(2)}) copy-start(s32[1152]{0:T(1024)} %param.10) | copy-start | bytes 13828
  0.6 21.5 %copy-start.12 = (s32[3,1152]{1,0:T(4,128)S(1)}, s32[3,1152]{1,0:T(4,128)}, u32[]{:S(2)}) copy-start(s32[3,1152]{1,0:T(4,128)} %param.11) | copy-start | bytes 41476
  2.5 21.0 %copy-start.13 = (f32[3,1152]{1,0:T(4,128)S(1)}, f32[3,1152]{1,0:T(4,128)}, u32[]{:S(2)}) copy-start(f32[3,1152]{1,0:T(4,128)} %param.12) | copy-start | bytes 41476
  2.5 107.5 %collective-permute-start = (f32[3,2,64,128]{3,2,1,0:T(8,128)}, f32[3,2,64,128]{3,2,1,0:T(8,128)}, u32[]{:S(2)}, u32[]{:S(2)}) collective-permute-start(f32[3,2,64,128]{3,2,1,0:T(8,128)} %get-tuple-element.33), channel_id=1, source_target_pairs={{0,2},{2,4},{4,6},{6,8},{8,10},{10,12},{12,14},{14,16},{16,18},{18... | collective-permute-start | bytes 589832 | tf_op jit(solution)/shard_map/ppermute | solution.py:22
  4.5 107.0 %collective-permute-start.1 = (f32[3,2,64,128]{3,2,1,0:T(8,128)}, f32[3,2,64,128]{3,2,1,0:T(8,128)}, u32[]{:S(2)}, u32[]{:S(2)}) collective-permute-start(f32[3,2,64,128]{3,2,1,0:T(8,128)} %get-tuple-element.32), channel_id=1, source_target_pairs={{2,0},{4,2},{6,4},{8,6},{10,8},{12,10},{14,12},{16,14},{18,16},{20... | collective-permute-start | bytes 589832 | tf_op jit(solution)/shard_map/ppermute | solution.py:23
  9.9 15.4 %copy-start = (f32[3,16,64,128]{3,2,1,0:T(8,128)S(1)}, f32[3,16,64,128]{3,2,1,0:T(8,128)}, u32[]{:S(2)}) copy-start(f32[3,16,64,128]{3,2,1,0:T(8,128)} %param.9) | copy-start | bytes 4718596
  9.9 108.9 %collective-permute-start.4 = (f32[3,2,64,128]{3,2,1,0:T(8,128)}, f32[3,2,64,128]{3,2,1,0:T(8,128)}, u32[]{:S(2)}, u32[]{:S(2)}) collective-permute-start(f32[3,2,64,128]{3,2,1,0:T(8,128)} %get-tuple-element.35), channel_id=1, source_target_pairs={{0,2},{2,4},{4,6},{6,8},{8,10},{10,12},{12,14},{14,16},{16,18},{18... | collective-permute-start | bytes 589832 | tf_op jit(solution)/shard_map/ppermute | solution.py:22
  11.9 108.5 %collective-permute-start.5 = (f32[3,2,64,128]{3,2,1,0:T(8,128)S(1)}, f32[3,2,64,128]{3,2,1,0:T(8,128)}, u32[]{:S(2)}, u32[]{:S(2)}) collective-permute-start(f32[3,2,64,128]{3,2,1,0:T(8,128)S(1)} %get-tuple-element.34), channel_id=1, source_target_pairs={{2,0},{4,2},{6,4},{8,6},{10,8},{12,10},{14,12},{16,14},{18,16},{20... | collective-permute-start | bytes 589832 | tf_op jit(solution)/shard_map/ppermute | solution.py:23
  31.6 66.4 %copy-start.14 = (f32[1152]{0:T(1024)S(1)}, f32[1152]{0:T(1024)}, u32[]{:S(2)}) copy-start(f32[1152]{0:T(1024)} %param.14) | copy-start | bytes 13828
  31.6 66.4 %copy-start.15 = (f32[1152]{0:T(1024)S(1)}, f32[1152]{0:T(1024)}, u32[]{:S(2)}) copy-start(f32[1152]{0:T(1024)} %param.13) | copy-start | bytes 13828
  31.6 66.8 %copy-start.2 = (f32[3,16,64,128]{3,2,1,0:T(8,128)S(1)}, f32[3,16,64,128]{3,2,1,0:T(8,128)}, u32[]{:S(2)}) copy-start(f32[3,16,64,128]{3,2,1,0:T(8,128)} %param.8) | copy-start | bytes 4718596
  112.7 16.6 %copy-start.3 = (f32[3,20,64,128]{3,2,1,0:T(8,128)}, f32[3,20,64,128]{3,2,1,0:T(8,128)S(1)}, u32[]{:S(2)}) copy-start(f32[3,20,64,128]{3,2,1,0:T(8,128)S(1)} %get-tuple-element.53) | copy-start | bytes 5898244
  112.8 14.8 %collective-permute-start.2 = (f32[3,20,2,128]{3,2,1,0:T(2,128)S(1)}, f32[3,20,2,128]{3,2,1,0:T(2,128)S(1)}, u32[]{:S(2)}, u32[]{:S(2)}) collective-permute-start(f32[3,20,2,128]{3,2,1,0:T(2,128)S(1)} %get-tuple-element.13), channel_id=1, source_target_pairs={{0,1},{2,3},{4,5},{6,7},{8,9},{10,11},{12,13},{14,15},{16,17},{18,... | collective-permute-start | bytes 184328 | tf_op jit(solution)/shard_map/ppermute | solution.py:22
  114.1 13.5 %collective-permute-start.3 = (f32[3,20,2,128]{3,2,1,0:T(2,128)S(1)}, f32[3,20,2,128]{3,2,1,0:T(2,128)S(1)}, u32[]{:S(2)}, u32[]{:S(2)}) collective-permute-start(f32[3,20,2,128]{3,2,1,0:T(2,128)S(1)} %get-tuple-element.14), channel_id=1, source_target_pairs={{1,0},{3,2},{5,4},{7,6},{9,8},{11,10},{13,12},{15,14},{17,16},{19,... | collective-permute-start | bytes 184328 | tf_op jit(solution)/shard_map/ppermute | solution.py:23
  120.4 13.7 %copy-start.11 = (f32[3,18,64,128]{3,2,1,0:T(8,128)}, f32[3,18,64,128]{3,2,1,0:T(8,128)S(1)}, u32[]{:S(2)}) copy-start(f32[3,18,64,128]{3,2,1,0:T(8,128)S(1)} %get-tuple-element.29) | copy-start | bytes 5308420
  121.6 7.7 %copy-start.7 = (f32[3,18,64,128]{3,2,1,0:T(8,128)}, f32[3,18,64,128]{3,2,1,0:T(8,128)S(1)}, u32[]{:S(2)}) copy-start(f32[3,18,64,128]{3,2,1,0:T(8,128)S(1)} %get-tuple-element.56) | copy-start | bytes 5308420
  121.6 8.9 %copy-start.4 = (f32[3,20,64,128]{3,2,1,0:T(8,128)}, f32[3,20,64,128]{3,2,1,0:T(8,128)S(1)}, u32[]{:S(2)}) copy-start(f32[3,20,64,128]{3,2,1,0:T(8,128)S(1)} %get-tuple-element.57) | copy-start | bytes 5898244
  121.7 8.8 %collective-permute-start.6 = (f32[3,20,2,128]{3,2,1,0:T(2,128)S(1)}, f32[3,20,2,128]{3,2,1,0:T(2,128)S(1)}, u32[]{:S(2)}, u32[]{:S(2)}) collective-permute-start(f32[3,20,2,128]{3,2,1,0:T(2,128)S(1)} %get-tuple-element.15), channel_id=1, source_target_pairs={{0,1},{2,3},{4,5},{6,7},{8,9},{10,11},{12,13},{14,15},{16,17},{18,... | collective-permute-start | bytes 184328 | tf_op jit(solution)/shard_map/ppermute | solution.py:22
  123.0 7.5 %collective-permute-start.7 = (f32[3,20,2,128]{3,2,1,0:T(2,128)S(1)}, f32[3,20,2,128]{3,2,1,0:T(2,128)S(1)}, u32[]{:S(2)}, u32[]{:S(2)}) collective-permute-start(f32[3,20,2,128]{3,2,1,0:T(2,128)S(1)} %get-tuple-element.16), channel_id=1, source_target_pairs={{1,0},{3,2},{5,4},{7,6},{9,8},{11,10},{13,12},{15,14},{17,16},{19,... | collective-permute-start | bytes 184328 | tf_op jit(solution)/shard_map/ppermute | solution.py:23
  134.1 20.6 %copy-start.5 = (f32[16,64,128]{2,1,0:T(8,128)S(1)}, f32[16,64,128]{2,1,0:T(8,128)}, u32[]{:S(2)}) copy-start(f32[16,64,128]{2,1,0:T(8,128)} %get-tuple-element.21) | copy-start | bytes 1572868
  161.1 7.1 %collective-permute-start.8 = (f32[3,2,64,128]{3,2,1,0:T(8,128)S(1)}, f32[3,2,64,128]{3,2,1,0:T(8,128)S(1)}, u32[]{:S(2)}, u32[]{:S(2)}) collective-permute-start(f32[3,2,64,128]{3,2,1,0:T(8,128)S(1)} %get-tuple-element.19), channel_id=1, source_target_pairs={{2,0},{4,2},{6,4},{8,6},{10,8},{12,10},{14,12},{16,14},{18,16},{20... | collective-permute-start | bytes 589832 | tf_op jit(solution)/shard_map/ppermute | solution.py:23
  163.1 10.3 %collective-permute-start.9 = (f32[3,2,64,128]{3,2,1,0:T(8,128)S(1)}, f32[3,2,64,128]{3,2,1,0:T(8,128)S(1)}, u32[]{:S(2)}, u32[]{:S(2)}) collective-permute-start(f32[3,2,64,128]{3,2,1,0:T(8,128)S(1)} %get-tuple-element.20), channel_id=1, source_target_pairs={{0,2},{2,4},{4,6},{6,8},{8,10},{10,12},{12,14},{14,16},{16,18},{18... | collective-permute-start | bytes 589832 | tf_op jit(solution)/shard_map/ppermute | solution.py:22
  174.8 6.1 %collective-permute-start.10 = (f32[3,16,2,128]{3,2,1,0:T(2,128)S(1)}, f32[3,16,2,128]{3,2,1,0:T(2,128)S(1)}, u32[]{:S(2)}, u32[]{:S(2)}) collective-permute-start(f32[3,16,2,128]{3,2,1,0:T(2,128)S(1)} %get-tuple-element.17), channel_id=1, source_target_pairs={{1,0},{3,2},{5,4},{7,6},{9,8},{11,10},{13,12},{15,14},{17,16},{19,... | collective-permute-start | bytes 147464 | tf_op jit(solution)/shard_map/ppermute | solution.py:23
  177.9 6.0 %collective-permute-start.11 = (f32[3,16,2,128]{3,2,1,0:T(2,128)S(1)}, f32[3,16,2,128]{3,2,1,0:T(2,128)S(1)}, u32[]{:S(2)}, u32[]{:S(2)}) collective-permute-start(f32[3,16,2,128]{3,2,1,0:T(2,128)S(1)} %get-tuple-element.18), channel_id=1, source_target_pairs={{0,1},{2,3},{4,5},{6,7},{8,9},{10,11},{12,13},{14,15},{16,17},{18,... | collective-permute-start | bytes 147464 | tf_op jit(solution)/shard_map/ppermute | solution.py:22
  (9 other events, 35.2 us)
